TPU v7x, 16 devices: a 4x2x1 block of a 4x4x8 slice. The times are simulated.
16 devices in a mesh: dp: 2 (over y, z), sp: 8 (over x, core).
Axes of the slice: x: 4, y: 2, z: 1, core: 2. Of those that a mesh axis runs over, the one named last changes fastest.
The devices are a block of a 4x4x8 slice.
Arguments:
- tokens: bfloat16 [256, 6144], P('dp'), parts along dimension 0
- w_query: bfloat16 [6144, 6144], replicated
- w_key: bfloat16 [6144, 128], replicated
- w_value: bfloat16 [6144, 128], replicated
- w_out: bfloat16 [6144, 6144], P('sp')
- k_cache: bfloat16 [256, 4096, 128], P('dp', 'sp'), parts along dimension 0
- v_cache: bfloat16 [256, 4096, 128], P('dp', 'sp'), parts along dimension 0
- positions: int32 [256], P('dp'), parts along dimension 0
Outputs:
- output 1: bfloat16 [256, 6144], P('dp'), parts along dimension 0
- output 2: bfloat16 [256, 4096, 128], P('dp', 'sp'), parts along dimension 0
- output 3: bfloat16 [256, 4096, 128], P('dp', 'sp'), parts along dimension 0
There are 2 independent parts. A program takes and returns all parts, laid end to end along the dimension named above; an argument that names none is the same for every part.
All inputs are finite; a program needn't handle non-finite values.
Results may differ from a plain program's by a relative error of at most 0.00432717.
Values are sent between devices in bfloat16 or wider.
A program may use at most 768 MiB of HBM per device.

v0:
```python
import jax
import jax.numpy as jnp
from jax import lax
from jax.sharding import PartitionSpec as P


def solution(mesh):
    def local_step(tokens, w_query, w_key, w_value, w_out, k_cache, v_cache, positions):
        n_rows, seq_local, head_dim = k_cache.shape
        q_width = w_query.shape[1]
        n_heads = q_width // head_dim
        rows_local = w_out.shape[0]
        shard_idx = lax.axis_index('sp')
        queries = jnp.dot(tokens, w_query, preferred_element_type=jnp.float32).astype(jnp.bfloat16).reshape(n_rows, n_heads, head_dim)
        key_new = jnp.dot(tokens, w_key, preferred_element_type=jnp.float32).astype(jnp.bfloat16)
        value_new = jnp.dot(tokens, w_value, preferred_element_type=jnp.float32).astype(jnp.bfloat16)
        local_pos = positions - shard_idx * seq_local
        slot_ids = jnp.arange(seq_local)
        hit_mask = (slot_ids[None, :] == local_pos[:, None])[:, :, None]
        k_upd = jnp.where(hit_mask, key_new[:, None, :], k_cache)
        v_upd = jnp.where(hit_mask, value_new[:, None, :], v_cache)
        scores = jnp.einsum('bhd,btd->bht', queries, k_upd, preferred_element_type=jnp.float32) * head_dim ** -0.5
        valid_mask = (slot_ids[None, :] <= local_pos[:, None])[:, None, :]
        scores = jnp.where(valid_mask, scores, -jnp.inf)
        row_peak = jnp.maximum(jnp.max(scores, axis=2), -1e30)
        weights = jnp.exp(scores - row_peak[:, :, None])
        weight_sum = jnp.sum(weights, axis=2)
        value_sum = jnp.einsum('bht,btd->bhd', weights.astype(jnp.bfloat16), v_upd, preferred_element_type=jnp.float32)
        peak_all = lax.pmax(row_peak, 'sp')
        rescale = jnp.exp(row_peak - peak_all)
        weight_all = lax.psum(weight_sum * rescale, 'sp')
        value_all = lax.psum(value_sum * rescale[:, :, None], 'sp')
        attn_heads = (value_all / weight_all[:, :, None]).astype(jnp.bfloat16).reshape(n_rows, q_width)
        attn_local = lax.dynamic_slice_in_dim(attn_heads, shard_idx * rows_local, rows_local, axis=1)
        partial = jnp.dot(attn_local, w_out, preferred_element_type=jnp.float32)
        attn_out = lax.psum(partial, 'sp').astype(jnp.bfloat16)
        return attn_out, k_upd, v_upd

    cache_spec = P('dp', 'sp', None)
    return jax.shard_map(local_step, mesh=mesh, in_specs=(P('dp', None), P(), P(), P(), P('sp', None), cache_spec, cache_spec, P('dp')), out_specs=(P('dp', None), cache_spec, cache_spec), check_vma=False)
```

profile of v0, /device:TPU:113, one launch (start us, length us, event | category | flops | bytes accessed | tf_op | source)
XLA Modules:
  0.0 252.8 jit_solution(8987497522190405648)
XLA Ops:
  7.2 0.0 copy-start
  7.2 0.1 all-reduce.3.cloned.1.call-start
  7.3 1.3 copy-done
  8.6 2.0 convolution_convert_fusion.2
  10.6 2.0 convolution_convert_fusion.1
  12.5 0.7 broadcast_subtract_fusion
  13.2 0.1 iota_compare_fusion.1
  13.4 26.4 %fusion.12 = bf16[16,8,48,128]{3,1,2,0:T(8,128)(2,1)S(1)} fusion(bf16[128,6144]{1,0:T(8,128)(2,1)S(1)} %copy-done, bf16[6144,6144]{1,0:T(8,128)(2,1)} %param.9), kind=kOutput, calls=%fused_computation.16 | convolution fusion | flops 9664462848 | bytes 78643200 | tf_op jit(solution)/shard_map/dot_general | solution.py:14
  39.8 0.4 copy.11
  40.1 23.3 %broadcast_select_fusion.1 = (bf16[128,512,128]{2,1,0:T(8,128)(2,1)}, bf16[128,512,128]{2,1,0:T(8,128)(2,1)}) fusion(bf16[128,512,128]{2,1,0:T(8,128)(2,1)} %param.13, pred[128,512]{1,0:T(8,128)(4,1)S(1)} %get-tuple-element.8, bf16[128,128]{1,0:T(8,128)(2,1)S(1)} %convolution_convert_fusion.2, bf16[128,512,128]{2,1,0:T(8,128)(2,1)} %param.14, ...), kind=kLoop, calls=%fused_computation.1 | loop fusion | flops 16777216 | bytes 67239936 | tf_op jit(solution)/shard_map/jit(_where)/select_n | solution.py:20
  63.4 12.2 %fusion = (f32[128,48]{1,0:T(8,128)S(1)}, f32[128,48,512]{2,1,0:T(8,128)}) fusion(pred[128,512]{1,0:T(8,128)(4,1)S(1)} %get-tuple-element.7, bf16[128,48,128]{2,1,0:T(8,128)(2,1)S(1)} %bitcast.18, bf16[128,512,128]{2,1,0:T(8,128)(2,1)} %get-tuple-element.5), kind=kOutput, calls=%fused_computation.4 | convolution fusion | flops 814737408 | bytes 31023104 | tf_op jit(solution)/shard_map/bhd,btd->bht/dot_general | solution.py:22
  75.6 24.5 %pmax.7 = f32[128,48]{1,0:T(8,128)S(1)} all-reduce(f32[128,48]{1,0:T(8,128)S(1)} %broadcast_maximum_fusion), channel_id=1, replica_groups=mesh['dp'=2,'sp'=8] {'sp'}, use_global_device_ids=true, to_apply=%region_1.2 | all-reduce | flops 6144 | bytes 49152 | tf_op jit(solution)/shard_map/pmax | solution.py:29
  100.1 0.0 copy-start.2
  100.1 8.7 %fusion.1 = f32[128,48]{1,0:T(8,128)S(1)} fusion(f32[128,48,512]{2,1,0:T(8,128)} %get-tuple-element.10, f32[128,48]{1,0:T(8,128)S(1)} %broadcast_maximum_fusion, pred[128,512]{1,0:T(8,128)(4,1)S(1)} %get-tuple-element.7), kind=kLoop, calls=%fused_computation.5 | loop fusion | flops 12576768 | bytes 12697600 | tf_op jit(solution)/shard_map/reduce_sum | solution.py:27
  108.8 0.0 copy-done.2
  108.8 9.3 %fusion.9 = f32[128,48,128]{2,1,0:T(8,128)} fusion(bf16[128,512,128]{2,1,0:T(8,128)(2,1)} %get-tuple-element.6, f32[128,48,512]{2,1,0:T(8,128)S(1)} %copy-done.2, f32[128,48]{1,0:T(8,128)S(1)} %broadcast_maximum_fusion, pred[128,512]{1,0:T(8,128)(4,1)S(1)} %get-tuple-element.7, f32[128,48]{1,0:T(8,128)S(1)} %get-tuple-element.4), kind=kOutput, calls=%fused_computation.14 | convolution fusion | flops 818675712 | bytes 32620544 | tf_op jit(solution)/shard_map/bht,btd->bhd/dot_general | solution.py:28
  118.2 0.1 all-reduce.3.cloned.1.call-update
  118.2 25.3 %psum.22 = f32[128,48]{1,0:T(8,128)S(1)} all-reduce(f32[128,48]{1,0:T(8,128)S(1)} %get-tuple-element.3), channel_id=1, replica_groups=mesh['dp'=2,'sp'=8] {'sp'}, use_global_device_ids=true, to_apply=%region_4.5 | all-reduce | flops 6144 | bytes 49152 | tf_op jit(solution)/shard_map/psum | solution.py:31
  143.6 36.1 %all-reduce.3.cloned.1.call-done = f32[128,48,128]{2,1,0:T(8,128)} async-done(((f32[128,48,128]{2,1,0:T(8,128)}), f32[128,48,128]{2,1,0:T(8,128)}) %all-reduce.3.cloned.1.call-update) | async-done | bytes 3145744 | tf_op jit(solution)/shard_map/psum | solution.py:32
  179.7 2.4 divide_convert_fusion
  182.1 0.4 copy.14
  182.5 0.0 copy-start.1
  182.5 6.9 %fusion.13 = f32[128,6144]{1,0:T(8,128)} fusion(bf16[768,6144]{1,0:T(8,128)(2,1)} %param.12, bf16[128,6144]{1,0:T(8,128)(2,1)S(1)} %bitcast.19, s32[]{:T(128)S(6)} %select_n.17), kind=kOutput, calls=%fused_computation.21 | convolution fusion | flops 1207959552 | bytes 12779524 | tf_op jit(solution)/shard_map/dot_general | solution.py:35
  189.4 56.5 %all-reduce.4 = bf16[128,6144]{1,0:T(8,128)(2,1)} all-reduce(f32[128,6144]{1,0:T(8,128)} %fusion.13), channel_id=1, replica_groups=mesh['dp'=2,'sp'=8] {'sp'}, use_global_device_ids=true, to_apply=%region_5.6 | all-reduce | flops 786432 | bytes 4718592 | tf_op jit(solution)/shard_map/psum | solution.py:36
  245.9 0.0 copy-done.1
  (2 shorter events, 0.0 us)
Async XLA Ops:
  7.2 1.4 copy-start
  7.2 172.5 %all-reduce.3.cloned.1.call-start = ((), (), s32[]{:S(2)}) async-start(), calls=%async_computation | async-start | bytes 6291456 | tf_op jit(solution)/shard_map/psum | solution.py:32
  100.1 8.7 %copy-start.2 = (f32[128,48,512]{2,1,0:T(8,128)S(1)}, f32[128,48,512]{2,1,0:T(8,128)}, u32[]{:S(2)}) copy-start(f32[128,48,512]{2,1,0:T(8,128)} %get-tuple-element.10) | copy-start | bytes 37748740
  182.5 63.4 %copy-start.1 = (bf16[128,6144]{1,0:T(8,128)(2,1)S(1)}, bf16[128,6144]{1,0:T(8,128)(2,1)}, u32[]{:S(2)}) copy-start(bf16[128,6144]{1,0:T(8,128)(2,1)} %param.8) | copy-start | bytes 4718596
Sparse Core Ops, SparseCore 0:
  118.4 61.2 all-reduce.2
where the time goes:
time: 255 us; the launch traced here: 253 us
  blocking collectives  106 us (42%)
  matrix products  58.7 us (23%)
  waiting for transfers between devices  36.2 us (14%)
  other arithmetic  35.2 us (14%)
  between operations  14.2 us (6%)
    psum x1, blocking collectives, local_step(): attn_out = lax.psum(partial, 'sp').astype(jnp.bfloat16)  56.5 us
    psum x1, waiting for transfers between devices, local_step(): value_all = lax.psum(value_sum * rescale[:, :, None], 'sp')  36.1 us
    dot_general x1, matrix products, local_step(): jnp.dot(tokens, w_query, preferred_element_type=jnp.float32)  26.4 us
    psum x1, blocking collectives, local_step(): weight_all = lax.psum(weight_sum * rescale, 'sp')  25.3 us
    pmax x1, blocking collectives, local_step(): peak_all = lax.pmax(row_peak, 'sp')  24.5 us
    select_n x1, other arithmetic, local_step(): k_upd = jnp.where(hit_mask, key_new[:, None, :], k_cache)  23.3 us
    dot_general x1, matrix products, local_step(): jnp.einsum('bhd,btd->bht', queries, k_upd, preferred_element_type=jnp.flo...  12.2 us
    dot_general x1, matrix products, local_step(): jnp.einsum('bht,btd->bhd', weights.astype(jnp.bfloat16), v_upd, preferred...  9.34 us
  transfers between devices with their start and end apart: 1, of which 1 were waited for; matrix products, arithmetic and copies ran while one was open for 0% of the time, Pallas kernels for 0%

commit v1 on v0

v1 whole, which is shorter than its diff:
```python
import functools
import math

import jax
import jax.numpy as jnp
from jax import lax
from jax.experimental import pallas as pl
from jax.experimental.pallas import tpu as pltpu
from jax.sharding import PartitionSpec as P

MESH = pl.DeviceIdType.MESH
ANY = pl.BlockSpec(memory_space=pl.ANY)
VMEM = pl.BlockSpec(memory_space=pltpu.VMEM)
SMEM = pl.BlockSpec(memory_space=pltpu.SMEM)
F32 = jnp.float32
BF16 = jnp.bfloat16
LIMIT = 60 * 1024 * 1024
CHUNKS = 4
GROUP = 8


def dot_t(a, b):
    return lax.dot_general(a, b, (((1,), (1,)), ((), ())), preferred_element_type=F32)


def project_kernel(n_tiles, depth, x_ref, wq_ref, wk_ref, wv_ref, q_ref, kn_ref, vn_ref, wbuf, kvbuf, wsem, kvsem, ssem, rsem):
    me = lax.axis_index('sp')
    core = lax.rem(me, 2)
    partner = me + 1 - 2 * core
    width = wbuf.shape[2]
    heads = width // q_ref.shape[2]

    def load(tile, slot):
        col = pl.multiple_of((core * n_tiles + tile) * width, width)
        return pltpu.make_async_copy(wq_ref.at[:, pl.ds(col, width)], wbuf.at[slot], wsem.at[slot])

    kv_loads = [pltpu.make_async_copy(w, kvbuf.at[i], kvsem.at[i]) for i, w in enumerate((wk_ref, wv_ref))]
    for tile in range(depth):
        load(tile, tile).start()
    barrier = pltpu.get_barrier_semaphore()
    pl.semaphore_signal(barrier, inc=1, device_id={'sp': partner}, device_id_type=MESH)
    pl.semaphore_wait(barrier, 1)

    def send(tile):
        head = (core * n_tiles + tile) * heads
        block = q_ref.at[pl.ds(head, heads)]
        return pltpu.make_async_remote_copy(block, block, ssem.at[tile], rsem.at[tile], device_id={'sp': partner}, device_id_type=MESH)

    def body(tile, carry):
        slot = lax.rem(tile, depth)
        load(tile, slot).wait()
        out = jnp.dot(x_ref[...], wbuf[slot], preferred_element_type=F32).astype(BF16)
        head = (core * n_tiles + tile) * heads
        for h in range(heads):
            q_ref[head + h] = out[:, h * q_ref.shape[2]:(h + 1) * q_ref.shape[2]]

        @pl.when(tile + depth < n_tiles)
        def _():
            load(tile + depth, slot).start()
        send(tile).start()
        return carry

    lax.fori_loop(0, n_tiles, body, 0)
    for c in kv_loads:
        c.start()
    for c, i, out in zip(kv_loads, range(2), (kn_ref, vn_ref)):
        c.wait()
        out[...] = jnp.dot(x_ref[...], kvbuf[i], preferred_element_type=F32).astype(BF16)

    def finish(tile, carry):
        send(tile).wait_send()
        head = ((1 - core) * n_tiles + tile) * heads
        block = q_ref.at[pl.ds(head, heads)]
        pltpu.make_async_remote_copy(block, block, ssem.at[tile], rsem.at[tile], device_id={'sp': partner}, device_id_type=MESH).wait_recv()
        return carry

    lax.fori_loop(0, n_tiles, finish, 0)


def attend_kernel(n_heads, scale, pos_ref, q_ref, kn_ref, vn_ref, k_ref, v_ref, ko_ref, vo_ref, o_ref, st_ref,
                  kbuf, vbuf, qs, osc, knf, vnf, mst, lst, isem, wsem, osem):
    me = lax.axis_index('sp')
    slots, group, seq, dim = kbuf.shape
    n_rows = pos_ref.shape[0]
    n_blocks = n_rows // group
    first = me * seq
    knf[...] = kn_ref[...].astype(F32)
    vnf[...] = vn_ref[...].astype(F32)
    mst[...] = jnp.zeros_like(mst)
    lst[...] = jnp.zeros_like(lst)

    def rows(i):
        return pl.ds(i * group, group)

    def load(i, s):
        return (pltpu.make_async_copy(k_ref.at[rows(i)], kbuf.at[s], isem.at[0, s]),
                pltpu.make_async_copy(v_ref.at[rows(i)], vbuf.at[s], isem.at[1, s]))

    def store(i, s):
        return (pltpu.make_async_copy(kbuf.at[s], ko_ref.at[rows(i)], wsem.at[0, s]),
                pltpu.make_async_copy(vbuf.at[s], vo_ref.at[rows(i)], wsem.at[1, s]))

    def put(i, s):
        return pltpu.make_async_copy(osc.at[s], o_ref.at[i], osem.at[s])

    ahead = slots // 2
    for i in range(ahead):
        for c in load(i, i):
            c.start()
    lane = lax.broadcasted_iota(jnp.int32, (1, seq), 1)
    lane_b = lax.broadcasted_iota(jnp.int32, (1, n_rows), 1)
    sub = lax.broadcasted_iota(jnp.int32, (16, dim), 0)

    def body(i, carry):
        s = lax.rem(i, slots)
        oslot = lax.rem(i, 2)
        for c in load(i, s):
            c.wait()

        @pl.when(i + ahead < n_blocks)
        def _():
            nxt = lax.rem(i + ahead, slots)

            @pl.when(i + ahead >= slots)
            def _():
                for c in store(i + ahead - slots, nxt):
                    c.wait()
            for c in load(i + ahead, nxt):
                c.start()

        @pl.when(i >= 2)
        def _():
            put(i - 2, oslot).wait()
        qs[...] = q_ref[:, rows(i), :].astype(F32).reshape(qs.shape)
        local = []
        for j in range(group):
            b = i * group + j
            p = pos_ref[b] - first
            local.append(p)
            pc = jnp.clip(p, 0, seq - 1)
            base = pl.multiple_of((pc // 16) * 16, 16)
            hit = (sub == pc - base) & (p >= 0) & (p < seq)
            for new, buf in ((knf, kbuf), (vnf, vbuf)):
                tile = buf[s, j, pl.ds(base, 16), :].astype(F32)
                buf[s, j, pl.ds(base, 16), :] = jnp.where(hit, new[pl.ds(b, 1), :], tile).astype(BF16)
        m_all, l_all = mst[...], lst[...]
        for j in range(group):
            b = i * group + j
            q = qs[pl.ds(j, n_heads, stride=group), :].astype(BF16)
            sc = jnp.where(lane <= local[j], dot_t(q, kbuf[s, j]), -jnp.inf)
            m = jnp.maximum(jnp.max(sc, axis=1, keepdims=True), -1e30)
            w = jnp.exp2((sc - m) * scale)
            l = jnp.sum(w, axis=1, keepdims=True)
            o = jnp.dot(w.astype(BF16), vbuf[s, j], preferred_element_type=F32)
            osc[oslot, pl.ds(j, n_heads, stride=group), :] = o
            m_all = jnp.where(lane_b == b, m * scale, m_all)
            l_all = jnp.where(lane_b == b, l, l_all)
        mst[...] = m_all
        lst[...] = l_all
        for c in store(i, s):
            c.start()
        put(i, oslot).start()
        return carry

    lax.fori_loop(0, n_blocks, body, 0)
    for i in range(n_blocks - slots, n_blocks):
        for c in store(i, i % slots):
            c.wait()
    for i in (n_blocks - 2, n_blocks - 1):
        put(i, i % 2).wait()
    n_dev = st_ref.shape[0]
    per = n_heads // n_dev
    m_all, l_all = mst[...], lst[...]
    for d in range(n_dev):
        st_ref[d, :n_heads] = m_all
        st_ref[d, n_heads:] = jnp.zeros((st_ref.shape[1] - n_heads, n_rows), F32)
        st_ref[d, n_heads:n_heads + per] = l_all[per * d:per * (d + 1)]


def combine_kernel(n_dev, per, st_ref, o_hbm, wo_hbm, y_ref, o_buf, wo, st_in, fac, linv, ob,
                   o_pair, o_r1, o_l1, o_r2, o_l2, y_buf, y_pair, y_r1, y_l1, y_r2, y_l2,
                   lsem, st_s, st_r, os_s, os_r, ys_s, ys_r, ag_s, ag_r):
    me = lax.axis_index('sp')
    n_chips = n_dev // 2
    core = lax.rem(me, 2)
    other = 1 - core
    chip = me // 2
    partner = me + 1 - 2 * core
    rchip, lchip, xchip = (lax.rem(chip + r, n_chips) for r in (1, 3, 2))
    right, left = rchip * 2 + core, lchip * 2 + core
    opposite = xchip * 2 + core
    chunks, n8 = o_buf.shape[0], o_buf.shape[1]
    rows = n8 * GROUP
    n_heads = n_dev * per
    dim = o_buf.shape[-1]
    width = per * dim
    half_o, half_y = o_buf.shape[4] // 2, rows // 2

    load_o = [pltpu.make_async_copy(o_hbm.at[k], o_buf.at[k], lsem.at[k]) for k in range(chunks)]
    load_w = pltpu.make_async_copy(wo_hbm, wo, lsem.at[chunks])
    for c in load_o:
        c.start()
    load_w.start()
    barrier = pltpu.get_barrier_semaphore()
    for r in range(1, n_dev):
        pl.semaphore_signal(barrier, inc=1, device_id={'sp': lax.rem(me + r, n_dev)}, device_id_type=MESH)
    pl.semaphore_wait(barrier, n_dev - 1)

    def remote(src, dst, s, r, dev):
        return pltpu.make_async_remote_copy(src, dst, s, r, device_id={'sp': dev}, device_id_type=MESH)

    stats = []
    for r in range(1, n_dev):
        dev = lax.rem(me + r, n_dev)
        c = remote(st_ref.at[dev], st_in.at[r - 1], st_s.at[r - 1], st_r.at[r - 1], dev)
        c.start()
        stats.append(c)
    for c in stats:
        c.wait_recv()
    mine = st_ref[0, :n_heads]
    top = mine
    for r in range(n_dev - 1):
        top = jnp.maximum(top, st_in[r, :n_heads])
    fac[...] = jnp.concatenate([jnp.exp2(mine - top), jnp.zeros((fac.shape[1] - n_heads, fac.shape[0]), F32)], axis=0).T
    total = jnp.zeros((8, top.shape[1]), F32)
    for d in range(n_dev):
        def term(st, top_d):
            return st[n_heads:n_heads + per] * jnp.exp2(st[per * d:per * (d + 1)] - top_d)
        top_d = top[per * d:per * (d + 1)]
        part = st_ref[d, n_heads:n_heads + per] * jnp.exp2(mine[per * d:per * (d + 1)] - top_d)
        for r in range(n_dev - 1):
            part += term(st_in[r], top_d)
        part = jnp.concatenate([part, jnp.ones((8 - per, top.shape[1]), F32)], axis=0)
        total = jnp.where(me == d, part, total)
    linv[...] = jnp.concatenate([total, jnp.ones((linv.shape[1] - 8, linv.shape[0]), F32)], axis=0).T

    class Reduce:
        def __init__(self, half, pair_src, pair, r1, l1, r2, l2, s, r):
            self.half, self.pair_src, self.pair = half, pair_src, pair
            self.r1, self.l1, self.r2, self.l2, self.s, self.r = r1, l1, r2, l2, s, r

        def copies(self, k):
            h = functools.partial(self.half, k)
            s, r = self.s, self.r
            return dict(
                pair=lambda: remote(self.pair_src(k), self.pair.at[k], s.at[k, 0], r.at[k, 0], partner),
                r1=lambda: remote(h(xchip, 0), self.r1.at[k], s.at[k, 1], r.at[k, 1], right),
                l1=lambda: remote(h(xchip, 1), self.l1.at[k], s.at[k, 2], r.at[k, 2], left),
                r2a=lambda: remote(h(rchip, 1), self.r2.at[k, 1], s.at[k, 3], r.at[k, 3], right),
                l2a=lambda: remote(h(lchip, 0), self.l2.at[k, 0], s.at[k, 4], r.at[k, 4], left),
                r2b=lambda: remote(h(rchip, 0), self.r2.at[k, 0], s.at[k, 5], r.at[k, 5], right),
                l2b=lambda: remote(h(lchip, 1), self.l2.at[k, 1], s.at[k, 6], r.at[k, 6], left),
            )

        def first(self, k, pair_half):
            c = self.copies(k)
            c['pair']().wait_recv()
            for x, g, name in ((xchip, 0, 'r1'), (xchip, 1, 'l1'), (rchip, 1, 'r2a'), (lchip, 0, 'l2a'),
                               (rchip, 0, None), (lchip, 1, None), (chip, 0, None), (chip, 1, None)):
                self.half(k, x, g)[...] += pair_half(k, x, g)[...]
                if name:
                    c[name]().start()

        def second(self, k):
            c = self.copies(k)
            c['r1']().wait_recv()
            self.half(k, rchip, 0)[...] += self.r1[k]
            c['r2b']().start()
            c['l1']().wait_recv()
            self.half(k, lchip, 1)[...] += self.l1[k]
            c['l2b']().start()

        def third(self, k):
            c = self.copies(k)
            for name in ('r2a', 'l2a', 'r2b', 'l2b'):
                c[name]().wait_recv()

        def drain(self, k):
            for c in self.copies(k).values():
                c().wait_send()

    red_o = Reduce(lambda k, x, g: o_buf.at[k, :, x, core, pl.ds(g * half_o, half_o), :],
                   lambda k: o_buf.at[k, :, :, other], o_pair, o_r1, o_l1, o_r2, o_l2, os_s, os_r)
    red_y = Reduce(lambda k, x, g: y_buf.at[k, core, x, pl.ds(g * half_y, half_y), :],
                   lambda k: y_buf.at[k, other], y_pair, y_r1, y_l1, y_r2, y_l2, ys_s, ys_r)

    def o_pair_half(k, x, g):
        return o_pair.at[k, :, x, pl.ds(g * half_o, half_o), :]

    def y_pair_half(k, x, g):
        return y_pair.at[k, x, pl.ds(g * half_y, half_y), :]

    def scale_o(k):
        load_o[k].wait()

        def one(t, carry):
            f = fac[pl.ds(pl.multiple_of(k * rows + t * GROUP, GROUP), GROUP), :]
            for h in range(n_heads):
                x, c, j = h // (2 * per), (h // per) % 2, h % per
                o_buf[k, t, x, c, j * GROUP:(j + 1) * GROUP, :] = o_buf[k, t, x, c, j * GROUP:(j + 1) * GROUP, :] * f[:, h:h + 1]
            return carry
        lax.fori_loop(0, n8, one, 0)
        red_o.copies(k)['pair']().start()

    def project(k):
        red_o.third(k)
        for t in range(n8):
            inv = linv[pl.ds(k * rows + t * GROUP, GROUP), :]
            for j in range(per):
                g, jj = j // (per // 2), j % (per // 2)
                sl = pl.ds(jj * GROUP, GROUP)
                v = (o_buf[k, t, chip, core, j * GROUP:(j + 1) * GROUP, :] + o_r2[k, g, t, sl, :]) + o_l2[k, g, t, sl, :]
                ob[t * GROUP:(t + 1) * GROUP, j * dim:(j + 1) * dim] = v / inv[:, j:j + 1]
        if k == 0:
            load_w.wait()
        a = ob[...].astype(BF16)
        for c in (other, core):
            def one(x, carry):
                col = pl.multiple_of((x * 2 + c) * width, width)
                y_buf[k, c, x] = jnp.dot(a, wo[:, pl.ds(col, width)], preferred_element_type=F32)
                return carry
            lax.fori_loop(0, n_chips, one, 0)
            if c is other:
                red_y.copies(k)['pair']().start()

    def y_block(k, dev, g=None):
        r = pl.ds(k * rows, rows) if g is None else pl.ds(k * rows + g * half_y, half_y)
        return y_ref.at[r, pl.ds(pl.multiple_of(dev * width, width), width)]

    def ag(k):
        s, r = ag_s, ag_r

        def to(block, i, dev):
            return lambda: remote(block, block, s.at[k, i], r.at[k, i], dev)
        return dict(
            own_r=to(y_block(k, me), 0, right), own_l=to(y_block(k, me), 1, left), own_p=to(y_block(k, me), 2, partner),
            fwd_r=to(y_block(k, left, 0), 3, right), fwd_l=to(y_block(k, right, 1), 4, left),
            left_p=to(y_block(k, left), 5, partner), right_p=to(y_block(k, right), 6, partner),
            opp_p0=to(y_block(k, opposite, 0), 7, partner), opp_p1=to(y_block(k, opposite, 1), 8, partner))

    def ag_in(k):
        s, r = ag_s, ag_r
        flip = lambda dev: dev + 1 - 2 * core

        def at(block, i):
            return lambda: remote(block, block, s.at[k, i], r.at[k, i], partner)
        return dict(
            left=at(y_block(k, left), 0), right=at(y_block(k, right), 1), own=at(y_block(k, partner), 2),
            opp0=at(y_block(k, opposite, 0), 3), opp1=at(y_block(k, opposite, 1), 4),
            left_p=at(y_block(k, flip(left)), 5), right_p=at(y_block(k, flip(right)), 6),
            opp_p0=at(y_block(k, flip(opposite), 0), 7), opp_p1=at(y_block(k, flip(opposite), 1), 8))

    def gather_start(k):
        red_y.third(k)
        for g in range(2):
            v = (y_buf[k, core, chip, g * half_y:(g + 1) * half_y, :] + y_r2[k, g]) + y_l2[k, g]
            y_block(k, me, g)[...] = v.astype(BF16)
        c = ag(k)
        for name in ('own_r', 'own_l', 'own_p'):
            c[name]().start()

    def gather_forward(k):
        c, i = ag(k), ag_in(k)
        i['left']().wait_recv()
        c['fwd_r']().start()
        c['left_p']().start()
        i['right']().wait_recv()
        c['fwd_l']().start()
        c['right_p']().start()

    def gather_opposite(k):
        c, i = ag(k), ag_in(k)
        for n in ('0', '1'):
            i['opp' + n]().wait_recv()
            c['opp_p' + n]().start()

    def gather_end(k):
        i = ag_in(k)
        for name in ('own', 'left_p', 'right_p', 'opp_p0', 'opp_p1'):
            i[name]().wait_recv()

    stages = [scale_o, lambda k: red_o.first(k, o_pair_half), red_o.second, project,
              lambda k: red_y.first(k, y_pair_half), red_y.second, gather_start, gather_forward, gather_opposite, gather_end]
    for t in range(chunks + len(stages) - 1):
        for s in reversed(range(len(stages))):
            if 0 <= t - s < chunks:
                stages[s](t - s)
    for c in stats:
        c.wait_send()
    for k in range(chunks):
        red_o.drain(k)
        red_y.drain(k)
        for c in ag(k).values():
            c().wait_send()


def solution(mesh):
    n_dev = mesh.shape['sp']

    def local_step(tokens, w_query, w_key, w_value, w_out, k_cache, v_cache, positions):
        n_rows, seq, dim = k_cache.shape
        d_model, q_width = w_query.shape
        n_heads = q_width // dim
        per = n_heads // n_dev
        width = 2 * dim
        n_tiles = q_width // width // 2
        depth = 3
        chunk = n_rows // CHUNKS
        n8 = chunk // GROUP
        dma = pltpu.SemaphoreType.DMA

        q, k_new, v_new = pl.pallas_call(
            functools.partial(project_kernel, n_tiles, depth),
            name='project',
            out_shape=[jax.ShapeDtypeStruct((n_heads, n_rows, dim), BF16)] + [jax.ShapeDtypeStruct((n_rows, dim), BF16)] * 2,
            in_specs=[VMEM, ANY, ANY, ANY], out_specs=[VMEM] * 3,
            scratch_shapes=[pltpu.VMEM((depth, d_model, width), BF16), pltpu.VMEM((2, d_model, dim), BF16),
                            dma((depth,)), dma((2,)), dma((n_tiles,)), dma((n_tiles,))],
            compiler_params=pltpu.CompilerParams(collective_id=0, has_side_effects=True, vmem_limit_bytes=LIMIT),
        )(tokens, w_query, w_key, w_value)

        slots = 4
        n_blocks = n_rows // GROUP
        k_out, v_out, o_part, stats = pl.pallas_call(
            functools.partial(attend_kernel, n_heads, dim ** -0.5 * math.log2(math.e)),
            name='attend',
            out_shape=[jax.ShapeDtypeStruct(k_cache.shape, BF16), jax.ShapeDtypeStruct(v_cache.shape, BF16),
                       jax.ShapeDtypeStruct((n_blocks, n_heads * GROUP, dim), F32),
                       jax.ShapeDtypeStruct((n_dev, n_heads + 8, n_rows), F32)],
            in_specs=[SMEM, VMEM, VMEM, VMEM, ANY, ANY], out_specs=[ANY, ANY, ANY, VMEM],
            scratch_shapes=[pltpu.VMEM((slots, GROUP, seq, dim), BF16), pltpu.VMEM((slots, GROUP, seq, dim), BF16),
                            pltpu.VMEM((n_heads * GROUP, dim), F32), pltpu.VMEM((2, n_heads * GROUP, dim), F32),
                            pltpu.VMEM((n_rows, dim), F32), pltpu.VMEM((n_rows, dim), F32),
                            pltpu.VMEM((n_heads, n_rows), F32), pltpu.VMEM((n_heads, n_rows), F32),
                            dma((2, slots)), dma((2, slots)), dma((2,))],
            compiler_params=pltpu.CompilerParams(vmem_limit_bytes=LIMIT),
        )(positions, q, k_new, v_new, k_cache, v_cache)

        n_chips = n_dev // 2
        o_view = o_part.reshape(CHUNKS, n8, n_chips, 2, per * GROUP, dim)
        ho, hy, out_w = per * GROUP // 2, chunk // 2, per * dim
        attn_out = pl.pallas_call(
            functools.partial(combine_kernel, n_dev, per),
            name='combine',
            out_shape=jax.ShapeDtypeStruct((n_rows, w_out.shape[1]), BF16),
            in_specs=[VMEM, ANY, ANY], out_specs=VMEM,
            scratch_shapes=[
                pltpu.VMEM(o_view.shape, F32), pltpu.VMEM(w_out.shape, BF16), pltpu.VMEM((n_dev - 1, n_heads + 8, n_rows), F32),
                pltpu.VMEM((n_rows, 128), F32), pltpu.VMEM((n_rows, 128), F32), pltpu.VMEM((chunk, out_w), F32),
                pltpu.VMEM((CHUNKS, n8, n_chips, per * GROUP, dim), F32),
                pltpu.VMEM((CHUNKS, n8, ho, dim), F32), pltpu.VMEM((CHUNKS, n8, ho, dim), F32),
                pltpu.VMEM((CHUNKS, 2, n8, ho, dim), F32), pltpu.VMEM((CHUNKS, 2, n8, ho, dim), F32),
                pltpu.VMEM((CHUNKS, 2, n_chips, chunk, out_w), F32), pltpu.VMEM((CHUNKS, n_chips, chunk, out_w), F32),
                pltpu.VMEM((CHUNKS, hy, out_w), F32), pltpu.VMEM((CHUNKS, hy, out_w), F32),
                pltpu.VMEM((CHUNKS, 2, hy, out_w), F32), pltpu.VMEM((CHUNKS, 2, hy, out_w), F32),
                dma((CHUNKS + 1,)), dma((n_dev - 1,)), dma((n_dev - 1,)),
                dma((CHUNKS, 7)), dma((CHUNKS, 7)), dma((CHUNKS, 7)), dma((CHUNKS, 7)), dma((CHUNKS, 9)), dma((CHUNKS, 9))],
            compiler_params=pltpu.CompilerParams(collective_id=1, has_side_effects=True, vmem_limit_bytes=LIMIT),
        )(stats, o_view, w_out)
        return attn_out, k_out, v_out

    cache_spec = P('dp', 'sp', None)
    return jax.shard_map(local_step, mesh=mesh, in_specs=(P('dp', None), P(), P(), P(), P('sp', None), cache_spec, cache_spec, P('dp')),
                         out_specs=(P('dp', None), cache_spec, cache_spec), check_vma=False)
```

time: 255 us -> 128 us (0.50)
  Pallas kernels: 0 us -> 124 us
  blocking collectives: 106 us -> 0 us
  matrix products: 58.7 us -> 0 us
  waiting for transfers between devices: 36.2 us -> 0 us
  other arithmetic: 35.2 us -> 0 us
  between operations: 14.2 us -> 0.65 us
    pallas_call x0 -> x3, Pallas kernels: none -> 124 us  [the longest x1 65.1 us: local_step(): pl.pallas_call(functools.partial(combine_kernel, n_dev, per), name='combi...]
    psum x2 -> x0, blocking collectives: 81.9 us -> none  [the longest x1 56.5 us: local_step(): attn_out = lax.psum(partial, 'sp').astype(jnp.bfloat16)]
    dot_general x6 -> x0, matrix products: 58.7 us -> none  [the longest x1 26.4 us: local_step(): jnp.dot(tokens, w_query, preferred_element_type=jnp.float32)]
    psum x1 -> x0, waiting for transfers between devices: 36.1 us -> none  [local_step(): value_all = lax.psum(value_sum * rescale[:, :, None], 'sp')]
    pmax x1 -> x0, blocking collectives: 24.5 us -> none  [local_step(): peak_all = lax.pmax(row_peak, 'sp')]
    select_n x1 -> x0, other arithmetic: 23.3 us -> none  [local_step(): k_upd = jnp.where(hit_mask, key_new[:, None, :], k_cache)]
    reduce_sum x1 -> x0, other arithmetic: 8.69 us -> none  [local_step(): weight_sum = jnp.sum(weights, axis=2)]
  transfers between devices with their start and end apart: 1 -> 0, of which waited for: 1 -> 0; matrix products, arithmetic and copies ran while one was open for 0% -> 0% of each run, Pallas kernels for 0% -> 0%
where the time goes in v1:
time: 128 us; the launch traced here: 127 us
  Pallas kernels  124 us (97%)
  local copies, waits for them, and re-layouts  2.69 us (2%)
    pallas_call x1, Pallas kernels, local_step(): pl.pallas_call(functools.partial(combine_kernel, n_dev, per), name='combi...  65.1 us
    pallas_call x1, Pallas kernels, local_step(): pl.pallas_call(functools.partial(attend_kernel, n_heads, dim ** (-0.5) *...  40.6 us
    pallas_call x1, Pallas kernels, local_step(): pl.pallas_call(functools.partial(project_kernel, n_tiles, depth), name='p...  18.3 us
    unnamed x1, local copies, waits for them, and re-layouts  2.69 us

profile of v1, /device:TPU:113, one launch (start us, length us, event | category | flops | bytes accessed | tf_op | source)
XLA Modules:
  0.0 127.4 jit_solution(7287784164835445849)
XLA Ops:
  0.6 18.3 %project.1 = (bf16[48,128,128]{2,1,0:T(8,128)(2,1)}, bf16[128,128]{1,0:T(8,128)(2,1)}, bf16[128,128]{1,0:T(8,128)(2,1)}) custom-call(bf16[128,6144]{1,0:T(8,128)(2,1)} %x_ref.1, bf16[6144,6144]{1,0:T(8,128)(2,1)} %wq_ref.1, bf16[6144,128]{1,0:T(8,128)(2,1)} %wk_ref.1, bf16[6144,128]{1,0:T(8,128)(2,1)} %wv_ref.1), custom_call_target="tpu_custom_call" | custom-call | tf_op jit(solution)/shard_map/project/pallas_call | solution.py:412
  18.9 40.6 %attend.1 = (bf16[128,512,128]{2,1,0:T(8,128)(2,1)}, bf16[128,512,128]{2,1,0:T(8,128)(2,1)}, f32[16,384,128]{2,1,0:T(8,128)}, f32[8,56,128]{2,1,0:T(8,128)}) custom-call(s32[128]{0:T(128)} %pos_ref.1, bf16[48,128,128]{2,1,0:T(8,128)(2,1)} %get-tuple-element.10.q_ref, bf16[128,128]{1,0:T(8,128)(2,1)} %get-tuple-element.11.kn_ref, ...), custom_call_target="tpu_custom_call" | custom-call | tf_op jit(solution)/shard_map/attend/pallas_call | solution.py:424
  59.6 65.1 %combine.1 = bf16[128,6144]{1,0:T(8,128)(2,1)} custom-call(f32[8,56,128]{2,1,0:T(8,128)} %get-tuple-element.13.st_ref, f32[4,4,4,2,48,128]{5,4,3,2,1,0:T(8,128)} %bitcast.1, bf16[768,6144]{1,0:T(8,128)(2,1)} %wo_hbm.1), custom_call_target="tpu_custom_call" | custom-call | tf_op jit(solution)/shard_map/combine/pallas_call | solution.py:442
  124.7 2.7 %copy.12 = bf16[128,6144]{1,0:T(8,128)(2,1)} copy(bf16[128,6144]{1,0:T(8,128)(2,1)} %combine.1) | data formatting | bytes 3145728

commit v2 on v1

--- a/solution.py
+++ b/solution.py
@@ -14,8 +14,8 @@
 SMEM = pl.BlockSpec(memory_space=pltpu.SMEM)
 F32 = jnp.float32
 BF16 = jnp.bfloat16
-LIMIT = 60 * 1024 * 1024
-CHUNKS = 4
+MIB = 1024 * 1024
+CHUNKS = 2
 GROUP = 8
 
 
@@ -78,7 +78,7 @@
 
 
 def attend_kernel(n_heads, scale, pos_ref, q_ref, kn_ref, vn_ref, k_ref, v_ref, ko_ref, vo_ref, o_ref, st_ref,
-                  kbuf, vbuf, qs, osc, knf, vnf, mst, lst, isem, wsem, osem):
+                  kbuf, vbuf, qs, scs, wts, osc, knf, vnf, mst, lst, isem, wsem, osem):
     me = lax.axis_index('sp')
     slots, group, seq, dim = kbuf.shape
     n_rows = pos_ref.shape[0]
@@ -143,18 +143,21 @@
             for new, buf in ((knf, kbuf), (vnf, vbuf)):
                 tile = buf[s, j, pl.ds(base, 16), :].astype(F32)
                 buf[s, j, pl.ds(base, 16), :] = jnp.where(hit, new[pl.ds(b, 1), :], tile).astype(BF16)
+        for j in range(group):
+            q = qs[pl.ds(j, n_heads, stride=group), :].astype(BF16)
+            scs[j] = dot_t(q, kbuf[s, j])
         m_all, l_all = mst[...], lst[...]
         for j in range(group):
             b = i * group + j
-            q = qs[pl.ds(j, n_heads, stride=group), :].astype(BF16)
-            sc = jnp.where(lane <= local[j], dot_t(q, kbuf[s, j]), -jnp.inf)
+            sc = jnp.where(lane <= local[j], scs[j], -jnp.inf)
             m = jnp.maximum(jnp.max(sc, axis=1, keepdims=True), -1e30)
             w = jnp.exp2((sc - m) * scale)
             l = jnp.sum(w, axis=1, keepdims=True)
-            o = jnp.dot(w.astype(BF16), vbuf[s, j], preferred_element_type=F32)
-            osc[oslot, pl.ds(j, n_heads, stride=group), :] = o
+            wts[j] = w.astype(BF16)
             m_all = jnp.where(lane_b == b, m * scale, m_all)
             l_all = jnp.where(lane_b == b, l, l_all)
+        for j in range(group):
+            osc[oslot, pl.ds(j, n_heads, stride=group), :] = jnp.dot(wts[j], vbuf[s, j], preferred_element_type=F32)
         mst[...] = m_all
         lst[...] = l_all
         for c in store(i, s):
@@ -416,7 +419,7 @@
             in_specs=[VMEM, ANY, ANY, ANY], out_specs=[VMEM] * 3,
             scratch_shapes=[pltpu.VMEM((depth, d_model, width), BF16), pltpu.VMEM((2, d_model, dim), BF16),
                             dma((depth,)), dma((2,)), dma((n_tiles,)), dma((n_tiles,))],
-            compiler_params=pltpu.CompilerParams(collective_id=0, has_side_effects=True, vmem_limit_bytes=LIMIT),
+            compiler_params=pltpu.CompilerParams(collective_id=0, has_side_effects=True, vmem_limit_bytes=20 * MIB),
         )(tokens, w_query, w_key, w_value)
 
         slots = 4
@@ -429,11 +432,12 @@
                        jax.ShapeDtypeStruct((n_dev, n_heads + 8, n_rows), F32)],
             in_specs=[SMEM, VMEM, VMEM, VMEM, ANY, ANY], out_specs=[ANY, ANY, ANY, VMEM],
             scratch_shapes=[pltpu.VMEM((slots, GROUP, seq, dim), BF16), pltpu.VMEM((slots, GROUP, seq, dim), BF16),
-                            pltpu.VMEM((n_heads * GROUP, dim), F32), pltpu.VMEM((2, n_heads * GROUP, dim), F32),
+                            pltpu.VMEM((n_heads * GROUP, dim), F32), pltpu.VMEM((GROUP, n_heads, seq), F32), pltpu.VMEM((GROUP, n_heads, seq), BF16),
+                            pltpu.VMEM((2, n_heads * GROUP, dim), F32),
                             pltpu.VMEM((n_rows, dim), F32), pltpu.VMEM((n_rows, dim), F32),
                             pltpu.VMEM((n_heads, n_rows), F32), pltpu.VMEM((n_heads, n_rows), F32),
                             dma((2, slots)), dma((2, slots)), dma((2,))],
-            compiler_params=pltpu.CompilerParams(vmem_limit_bytes=LIMIT),
+            compiler_params=pltpu.CompilerParams(vmem_limit_bytes=24 * MIB),
         )(positions, q, k_new, v_new, k_cache, v_cache)
 
         n_chips = n_dev // 2
@@ -455,7 +459,7 @@
                 pltpu.VMEM((CHUNKS, 2, hy, out_w), F32), pltpu.VMEM((CHUNKS, 2, hy, out_w), F32),
                 dma((CHUNKS + 1,)), dma((n_dev - 1,)), dma((n_dev - 1,)),
                 dma((CHUNKS, 7)), dma((CHUNKS, 7)), dma((CHUNKS, 7)), dma((CHUNKS, 7)), dma((CHUNKS, 9)), dma((CHUNKS, 9))],
-            compiler_params=pltpu.CompilerParams(collective_id=1, has_side_effects=True, vmem_limit_bytes=LIMIT),
+            compiler_params=pltpu.CompilerParams(collective_id=1, has_side_effects=True, vmem_limit_bytes=36 * MIB),
         )(stats, o_view, w_out)
         return attn_out, k_out, v_out
 

time: 128 us -> 104 us (0.81)
  Pallas kernels: 124 us -> 94.1 us
  local copies, waits for them, and re-layouts: 2.69 us -> 9.45 us
    pallas_call x1, Pallas kernels: 40.6 us -> 21.7 us  [local_step(): pl.pallas_call(functools.partial(attend_kernel, n_heads, dim ** (-0.5) *...]
    pallas_call x1, Pallas kernels: 65.1 us -> 56 us  [local_step(): pl.pallas_call(functools.partial(combine_kernel, n_dev, per), name='combi...]
    unnamed x1 -> x13, local copies, waits for them, and re-layouts: 2.69 us -> 9.45 us
    pallas_call x1, Pallas kernels: 18.3 us -> 16.4 us  [local_step(): pl.pallas_call(functools.partial(project_kernel, n_tiles, depth), name='p...]
where the time goes in v2:
time: 104 us
  Pallas kernels  94.1 us (90%)
  local copies, waits for them, and re-layouts  9.45 us (9%)
    pallas_call x1, Pallas kernels, local_step(): pl.pallas_call(functools.partial(combine_kernel, n_dev, per), name='combi...  56 us
    pallas_call x1, Pallas kernels, local_step(): pl.pallas_call(functools.partial(attend_kernel, n_heads, dim ** (-0.5) *...  21.7 us
    pallas_call x1, Pallas kernels, local_step(): pl.pallas_call(functools.partial(project_kernel, n_tiles, depth), name='p...  16.4 us
    unnamed x13, local copies, waits for them, and re-layouts  9.45 us

profile of v2, /device:TPU:113, one launch (start us, length us, event | category | flops | bytes accessed | tf_op | source)
XLA Modules:
  0.0 104.2 jit_solution(7762467290508459932)
XLA Ops:
  0.6 0.0 copy-start.2
  0.6 1.4 %copy-done.2 = bf16[128,6144]{1,0:T(8,128)(2,1)S(1)} copy-done((bf16[128,6144]{1,0:T(8,128)(2,1)S(1)}, bf16[128,6144]{1,0:T(8,128)(2,1)}, u32[]{:S(2)}) %copy-start.2) | copy-done | bytes 1572888
  2.0 0.0 copy-start.3
  2.0 1.4 %copy-done.3 = bf16[6144,128]{1,0:T(8,128)(2,1)S(1)} copy-done((bf16[6144,128]{1,0:T(8,128)(2,1)S(1)}, bf16[6144,128]{1,0:T(8,128)(2,1)}, u32[]{:S(2)}) %copy-start.3) | copy-done | bytes 1572888
  3.4 0.0 copy-start.4
  3.5 1.4 %copy-done.4 = bf16[6144,128]{1,0:T(8,128)(2,1)S(1)} copy-done((bf16[6144,128]{1,0:T(8,128)(2,1)S(1)}, bf16[6144,128]{1,0:T(8,128)(2,1)}, u32[]{:S(2)}) %copy-start.4) | copy-done | bytes 1572888
  4.9 0.0 copy-start
  4.9 0.0 copy-start.5
  4.9 16.4 %project.1 = (bf16[48,128,128]{2,1,0:T(8,128)(2,1)S(1)}, bf16[128,128]{1,0:T(8,128)(2,1)S(1)}, bf16[128,128]{1,0:T(8,128)(2,1)S(1)}) custom-call(bf16[128,6144]{1,0:T(8,128)(2,1)S(1)} %copy-done.2, bf16[6144,6144]{1,0:T(8,128)(2,1)} %wq_ref.1, bf16[6144,128]{1,0:T(8,128)(2,1)S(1)} %copy-done.3, bf16[6144,128]{1,0:T(8,128)(2,1)S(1)} %copy-done.4), custom_call_target="tpu_custom_call" | custom-call | tf_op jit(solution)/shard_map/project/pallas_call | solution.py:415
  21.2 0.4 copy-done
  21.6 0.0 copy-done.5
  21.6 21.7 %attend.1 = (bf16[128,512,128]{2,1,0:T(8,128)(2,1)}, bf16[128,512,128]{2,1,0:T(8,128)(2,1)}, f32[16,384,128]{2,1,0:T(8,128)S(1)}, f32[8,56,128]{2,1,0:T(8,128)S(1)}) custom-call(s32[128]{0:T(128)S(1)} %copy-done.5, bf16[48,128,128]{2,1,0:T(8,128)(2,1)S(1)} %get-tuple-element.10.q_ref, bf16[128,128]{1,0:T(8,128)(2,1)S(1)} %get-tuple-element.11.kn_ref, ...), custom_call_target="tpu_custom_call" | custom-call | tf_op jit(solution)/shard_map/attend/pallas_call | solution.py:427
  43.4 0.0 copy-start.1
  43.4 3.7 %copy-done.1 = bf16[768,6144]{1,0:T(8,128)(2,1)S(1)} copy-done((bf16[768,6144]{1,0:T(8,128)(2,1)S(1)}, bf16[768,6144]{1,0:T(8,128)(2,1)}, u32[]{:S(2)}) %copy-start.1) | copy-done | bytes 9437208
  47.0 56.0 %combine.1 = bf16[128,6144]{1,0:T(8,128)(2,1)S(1)} custom-call(f32[8,56,128]{2,1,0:T(8,128)S(1)} %get-tuple-element.13.st_ref, f32[2,8,4,2,48,128]{5,4,3,2,1,0:T(8,128)S(1)} %bitcast.1, bf16[768,6144]{1,0:T(8,128)(2,1)S(1)} %copy-done.1), custom_call_target="tpu_custom_call" | custom-call | tf_op jit(solution)/shard_map/combine/pallas_call | solution.py:446
  103.0 1.1 %copy.12 = bf16[128,6144]{1,0:T(8,128)(2,1)} copy(bf16[128,6144]{1,0:T(8,128)(2,1)S(1)} %combine.1) | data formatting | bytes 3145728
Async XLA Ops:
  0.6 1.4 %copy-start.2 = (bf16[128,6144]{1,0:T(8,128)(2,1)S(1)}, bf16[128,6144]{1,0:T(8,128)(2,1)}, u32[]{:S(2)}) copy-start(bf16[128,6144]{1,0:T(8,128)(2,1)} %x_ref.1) | copy-start | bytes 4718596
  2.0 1.4 %copy-start.3 = (bf16[6144,128]{1,0:T(8,128)(2,1)S(1)}, bf16[6144,128]{1,0:T(8,128)(2,1)}, u32[]{:S(2)}) copy-start(bf16[6144,128]{1,0:T(8,128)(2,1)} %wk_ref.1) | copy-start | bytes 4718596
  3.4 1.4 %copy-start.4 = (bf16[6144,128]{1,0:T(8,128)(2,1)S(1)}, bf16[6144,128]{1,0:T(8,128)(2,1)}, u32[]{:S(2)}) copy-start(bf16[6144,128]{1,0:T(8,128)(2,1)} %wv_ref.1) | copy-start | bytes 4718596
  4.9 16.8 %copy-start = (bf16[128,512,128]{2,1,0:T(8,128)(2,1)S(1)}, bf16[128,512,128]{2,1,0:T(8,128)(2,1)}, u32[]{:S(2)}) copy-start(bf16[128,512,128]{2,1,0:T(8,128)(2,1)} %k_ref.1) | copy-start | bytes 50331652
  4.9 16.8 %copy-start.5 = (s32[128]{0:T(128)S(1)}, s32[128]{0:T(128)}, u32[]{:S(2)}) copy-start(s32[128]{0:T(128)} %pos_ref.1) | copy-start | bytes 1540
  43.4 3.7 %copy-start.1 = (bf16[768,6144]{1,0:T(8,128)(2,1)S(1)}, bf16[768,6144]{1,0:T(8,128)(2,1)}, u32[]{:S(2)}) copy-start(bf16[768,6144]{1,0:T(8,128)(2,1)} %wo_hbm.1) | copy-start | bytes 28311556
